TPU v7x, 32 devices: a 4x2x2 block of a 4x4x8 slice. The times are simulated.
32 devices in a mesh: dp: 4 (over y, z), ep: 8 (over x, core).
Axes of the slice: x: 4, y: 2, z: 2, core: 2. Of those that a mesh axis runs over, the one named last changes fastest.
The devices are a block of a 4x4x8 slice.
Arguments:
- x_tok: bfloat16 [32, 512, 2048], P(('dp', 'ep')), parts along dimension 0
- w_query: bfloat16 [2048, 16, 128], P('ep')
- w_key: bfloat16 [2048, 16, 128], P('ep')
- w_value: bfloat16 [2048, 16, 128], P('ep')
- w_out: bfloat16 [2048, 2048], P('ep')
- w_router: float32 [2048, 64], replicated
- w_gate: bfloat16 [64, 2048, 1024], P('ep')
- w_up: bfloat16 [64, 2048, 1024], P('ep')
- w_down: bfloat16 [64, 1024, 2048], P('ep')
- ws_gate: bfloat16 [2048, 1024], P('ep')
- ws_up: bfloat16 [2048, 1024], P('ep')
- ws_down: bfloat16 [1024, 2048], P('ep')
- expert_ids: int32 [32, 512, 8], P(('dp', 'ep')), parts along dimension 0
Outputs:
- output: bfloat16 [32, 512, 2048], P(('dp', 'ep')), parts along dimension 0
There are 4 independent parts. A program takes and returns all parts, laid end to end along the dimension named above; an argument that names none is the same for every part.
All inputs are finite; a program needn't handle non-finite values.
Results may differ from a plain program's by a relative error of at most 0.0133186.
Values are sent between devices in bfloat16 or wider.
A program may use at most 768 MiB of HBM per device.

v0:
```python
import functools
import jax
import jax.numpy as jnp
from jax import lax
from jax.experimental import pallas as pl
from jax.experimental.pallas import tpu as pltpu
from jax.sharding import PartitionSpec as P

EPSILON = 1e-6
CAP_FACTOR = 2
ALIGN = 16
VMEM_BYTES = 60 * 1024 * 1024
MAX_VMEM = 67043328


def rms_norm(values):
    as_f32 = values.astype(jnp.float32)
    return as_f32 * lax.rsqrt(jnp.mean(as_f32 * as_f32, axis=-1, keepdims=True) + EPSILON)


def params(**kw):
    return pltpu.CompilerParams(vmem_limit_bytes=VMEM_BYTES, **kw)


def neighbour(chips, swap=False):
    me, group = lax.axis_index('ep'), lax.axis_size('ep')
    side = lax.rem(me, 2)
    chip = lax.rem(me // 2 + chips + group // 2, group // 2)
    return {'ep': chip * 2 + (1 - side if swap else side)}


def greet(*devices):
    barrier = pltpu.get_barrier_semaphore()
    for device in devices:
        pl.semaphore_signal(barrier, inc=1, device_id=device, device_id_type=pl.DeviceIdType.MESH)
    pl.semaphore_wait(barrier, len(devices))


def remote(src, dst, send_sem, recv_sem, device):
    return pltpu.make_async_remote_copy(src_ref=src, dst_ref=dst, send_sem=send_sem, recv_sem=recv_sem, device_id=device, device_id_type=pl.DeviceIdType.MESH)


class Gather:
    def __init__(self, buf, send, recv, split=True):
        other = neighbour(0, True)
        half = buf.shape[1] // 2
        lo, hi = pl.ds(0, half), pl.ds(half, half)

        def copy(k, src, dst, device):
            return remote(src, dst, send.at[k], recv.at[k], device)

        self.own = [copy(0, buf.at[0], buf.at[1], neighbour(1)), copy(1, buf.at[0], buf.at[2], neighbour(-1))]
        self.mate = [copy(2, buf.at[0], buf.at[4], other)]
        self.near_mate = [copy(3, buf.at[1], buf.at[5], other), copy(4, buf.at[2], buf.at[6], other)]
        if split:
            self.far = [copy(5, buf.at[1, lo], buf.at[3, lo], neighbour(1)), copy(6, buf.at[2, hi], buf.at[3, hi], neighbour(-1))]
            self.far_mate = [copy(7, buf.at[3, lo], buf.at[7, lo], other), copy(8, buf.at[3, hi], buf.at[7, hi], other)]
        else:
            self.far = [copy(5, buf.at[0], buf.at[3], neighbour(2))]
            self.far_mate = [copy(7, buf.at[3], buf.at[7], other)]
        self.split = split

    def begin(self):
        for copy in self.own + self.mate + ([] if self.split else self.far):
            copy.start()

    def forward(self):
        for k in range(2):
            self.own[k].wait_recv()
            if self.split:
                self.far[k].start()
            self.near_mate[k].start()

    def forward_far(self):
        for copy, mate in zip(self.far, self.far_mate):
            copy.wait_recv()
            mate.start()

    def arrive(self, copies):
        for copy in copies:
            copy.wait_recv()

    def finish(self):
        for copy in self.own + self.mate + self.near_mate + self.far + self.far_mate:
            copy.wait_send()


def owner(r):
    step = (0, -1, 1, 2)[r % 4]
    return neighbour(step, r >= 4)['ep']


def attention_layer_kernel(x_ref, ids_ref, k_hbm, v_hbm, q_hbm, o_hbm, h_ref, rank_ref, ids_out, w_buf, n_buf, qkv, acc, ids_buf, load_sems, send, recv, ids_send, ids_recv):
    n_tok, d_model = x_ref.shape
    group, local = rank_ref.shape[:2]
    size = d_model // group
    head = 128
    width = 512
    keys, vals, queries, outs = range(4)
    gathers = [Gather(w_buf.at[w], send.at[w], recv.at[w]) for w in range(4)]
    ids_gather = Gather(ids_buf, ids_send, ids_recv, split=False)
    loads = [pltpu.make_async_copy(ref, w_buf.at[w, 0], load_sems.at[w]) for w, ref in enumerate((k_hbm, v_hbm, q_hbm, o_hbm))]
    ids_load = pltpu.make_async_copy(ids_ref, ids_buf.at[0], load_sems.at[4])
    ids_load.start()
    for load in loads:
        load.start()
    greet(neighbour(1), neighbour(-1), neighbour(2), neighbour(0, True))
    ids_load.wait()
    ids_gather.begin()
    for w in (keys, vals):
        loads[w].wait()
        gathers[w].begin()

    @pl.loop(0, n_tok // 128)
    def _(i):
        rows = pl.ds(pl.multiple_of(i * 128, 128), 128)
        normed = rms_norm(x_ref[rows, :]).astype(jnp.bfloat16)
        qkv[0, rows, :] = normed
        for r in range(group):
            n_buf[rows, r * size:(r + 1) * size] = qkv[0, rows, pl.ds(pl.multiple_of(owner(r) * size, size), size)]

    ids_gather.arrive(ids_gather.own + ids_gather.mate)
    for copy in ids_gather.near_mate:
        copy.start()
    ids_gather.forward_far()
    ids_gather.arrive(ids_gather.near_mate + ids_gather.far_mate)
    first = lax.axis_index('ep') * local
    before = (lax.broadcasted_iota(jnp.int32, (n_tok, n_tok), 0) < lax.broadcasted_iota(jnp.int32, (n_tok, n_tok), 1)).astype(jnp.float32).astype(jnp.bfloat16)
    for r in range(group):
        member = jnp.concatenate([jnp.max((ids_buf[r] == first + e).astype(jnp.float32), axis=0, keepdims=True) for e in range(local)], axis=0)
        rank = jnp.dot(member.astype(jnp.bfloat16), before, preferred_element_type=jnp.float32)
        rank_ref[r] = jnp.where(member > 0.5, rank, -1.0).astype(jnp.int32)

    def project(w, store):
        @pl.loop(0, d_model // width)
        def _(c):
            cols = pl.ds(pl.multiple_of(c * width, width), width)
            weight = jnp.concatenate([w_buf[w, r, :, cols] for r in range(group)], axis=0)
            store(cols, jnp.dot(n_buf[...], weight, preferred_element_type=jnp.float32).astype(jnp.bfloat16))

    def keep(w):
        def store(cols, values):
            qkv[w, :, cols] = values
        return store

    def complete(w):
        gathers[w].forward_far()
        gathers[w].arrive(gathers[w].mate + gathers[w].near_mate + gathers[w].far_mate)

    def attend(lo, hi):
        for r in range(lo, hi):
            start = owner(r) * size

            @pl.loop(0, size // head)
            def _(k):
                cols = pl.ds(pl.multiple_of(start + k * head, head), head)
                parts = 2
                step = n_tok // parts
                for part in range(parts):
                    top, end = part * step, (part + 1) * step
                    scores = lax.dot_general(qkv[queries, top:end, cols], qkv[keys, :end, cols], (((1,), (1,)), ((), ())), preferred_element_type=jnp.float32) * (head ** -0.5)
                    row = top + lax.broadcasted_iota(jnp.int32, scores.shape, 0)
                    col = lax.broadcasted_iota(jnp.int32, scores.shape, 1)
                    scores = jnp.where(row >= col, scores, -1e30)
                    weights = jnp.exp(scores - jnp.max(scores, axis=-1, keepdims=True))
                    probs = (weights / jnp.sum(weights, axis=-1, keepdims=True)).astype(jnp.bfloat16)
                    n_buf[top:end, pl.ds(pl.multiple_of(r * size + k * head, head), head)] = jnp.dot(probs, qkv[vals, :end, cols], preferred_element_type=jnp.float32).astype(jnp.bfloat16)

    gathers[keys].forward()
    loads[queries].wait()
    gathers[queries].begin()
    gathers[vals].forward()
    complete(keys)
    project(keys, keep(keys))
    gathers[queries].forward()
    loads[outs].wait()
    gathers[outs].begin()
    complete(vals)
    project(vals, keep(vals))
    complete(queries)
    project(queries, keep(queries))
    attend(0, group // 2)
    gathers[outs].forward()
    attend(group // 2, group)
    gathers[outs].arrive(gathers[outs].mate + gathers[outs].near_mate)
    side = group // 2
    spans = [(r0 * size, (r0 + side - 1) * size) for r0 in (0, side)]

    @pl.loop(0, d_model // width)
    def _(c):
        cols = pl.ds(pl.multiple_of(c * width, width), width)
        weights = [jnp.concatenate([w_buf[outs, r, :, cols] for r in range(r0, r0 + side - 1)], axis=0) for r0 in (0, side)]
        parts = [jnp.dot(n_buf[:, lo:hi], weight, preferred_element_type=jnp.float32) for (lo, hi), weight in zip(spans, weights)]
        acc[:, cols] = parts[0] + parts[1]

    gathers[outs].forward_far()
    gathers[outs].arrive(gathers[outs].far_mate)

    @pl.loop(0, d_model // width)
    def _(c):
        cols = pl.ds(pl.multiple_of(c * width, width), width)
        parts = [jnp.dot(n_buf[:, hi:hi + size], w_buf[outs, hi // size, :, cols], preferred_element_type=jnp.float32) for lo, hi in spans]
        attn = (acc[:, cols] + parts[0] + parts[1]).astype(jnp.bfloat16)
        h_ref[:, cols] = (x_ref[:, cols].astype(jnp.float32) + attn.astype(jnp.float32)).astype(jnp.bfloat16)

    for r in range(group):
        ids_out[r] = ids_buf[r]
    for gather in gathers + [ids_gather]:
        gather.finish()


def attention_layer(x, ids_t, k_shard, v_shard, q_shard, o_shard, group, local):
    n_tok, d_model = x.shape
    top_k = ids_t.shape[0]
    vmem = pl.BlockSpec(memory_space=pltpu.VMEM)
    anywhere = pl.BlockSpec(memory_space=pl.ANY)
    return pl.pallas_call(
        attention_layer_kernel,
        in_specs=[vmem] + [anywhere] * 5,
        out_specs=[vmem] * 3,
        out_shape=[jax.ShapeDtypeStruct(x.shape, jnp.bfloat16), jax.ShapeDtypeStruct((group, local, n_tok), jnp.int32), jax.ShapeDtypeStruct((group, top_k, n_tok), jnp.int32)],
        scratch_shapes=[
            pltpu.VMEM((4, group) + k_shard.shape, jnp.bfloat16),
            pltpu.VMEM(x.shape, jnp.bfloat16),
            pltpu.VMEM((3,) + x.shape, jnp.bfloat16),
            pltpu.VMEM(x.shape, jnp.float32),
            pltpu.VMEM((group, top_k, n_tok), jnp.int32),
            pltpu.SemaphoreType.DMA((5,)),
            pltpu.SemaphoreType.DMA((4, 9)),
            pltpu.SemaphoreType.DMA((4, 9)),
            pltpu.SemaphoreType.DMA((9,)),
            pltpu.SemaphoreType.DMA((9,)),
        ],
        compiler_params=pltpu.CompilerParams(vmem_limit_bytes=MAX_VMEM, collective_id=0, has_side_effects=True),
        cost_estimate=pl.CostEstimate(flops=9 * n_tok * d_model * d_model, bytes_accessed=8 * d_model * d_model // group, transcendentals=0),
        name="attention_layer",
    )(x, ids_t, k_shard, v_shard, q_shard, o_shard)


def dispatch_kernel(h_ref, wr_ref, ids_ref, rank_ref, x_hbm, gates_ref, u_hbm, u_buf, pick, stage, g_buf, out_sems, send, recv, g_send, g_recv):
    n_tok, d_model = h_ref.shape
    group, local = rank_ref.shape[:2]
    capacity = x_hbm.shape[2]
    n_experts = wr_ref.shape[0]
    top_k = ids_ref.shape[0]
    width = stage.shape[3]
    n_cols = d_model // width
    tokens = Gather(u_buf, send, recv)
    gates = Gather(g_buf, g_send, g_recv, split=False)

    @pl.loop(0, n_tok // 128)
    def _(i):
        rows = pl.ds(pl.multiple_of(i * 128, 128), 128)
        u_buf[0, rows, :] = rms_norm(h_ref[rows, :]).astype(jnp.bfloat16)

    greet(neighbour(1), neighbour(-1), neighbour(2), neighbour(0, True))
    tokens.begin()
    keep = pltpu.make_async_copy(u_buf.at[0], u_hbm, out_sems.at[2])
    keep.start()

    for i in range(n_tok // 128):
        rows = slice(i * 128, (i + 1) * 128)
        logits = lax.dot_general(wr_ref[...], rms_norm(h_ref[rows, :]), (((1,), (1,)), ((), ())), precision=lax.Precision.HIGHEST, preferred_element_type=jnp.float32)
        experts_iota = lax.broadcasted_iota(jnp.int32, (n_experts, 128), 0)
        chosen = jnp.concatenate([jnp.sum(jnp.where(experts_iota == ids_ref[j:j + 1, rows], logits, 0.0), axis=0, keepdims=True) for j in range(top_k)], axis=0)
        weights = jnp.exp(chosen - jnp.max(chosen, axis=0, keepdims=True))
        g_buf[0, :, rows] = weights / jnp.sum(weights, axis=0, keepdims=True)
    gates.begin()

    def put(r, c, slot):
        cols = pl.ds(pl.multiple_of(c * width, width), width)
        return pltpu.make_async_copy(stage.at[slot], x_hbm.at[r, :, :, cols], out_sems.at[slot])

    def dispatch(r, before):
        slots = lax.broadcasted_iota(jnp.int32, (capacity, n_tok), 0)
        for e in range(local):
            pick[e * capacity:(e + 1) * capacity, :] = (rank_ref[r, e:e + 1, :] == slots).astype(jnp.float32).astype(jnp.bfloat16)

        @pl.loop(0, n_cols)
        def _(c):
            slot = lax.rem(c, 2)
            cols = pl.ds(pl.multiple_of(c * width, width), width)
            if before is None:
                @pl.when(c >= 2)
                def _():
                    put(r, c - 2, slot).wait()
            else:
                @pl.when(c >= 2)
                def _():
                    put(r, c - 2, slot).wait()

                @pl.when(c < 2)
                def _():
                    put(before, n_cols - 2 + c, slot).wait()
            rows = jnp.dot(pick[...], u_buf[r, :, cols], preferred_element_type=jnp.float32).astype(jnp.bfloat16)
            for e in range(local):
                stage[slot, e] = rows[e * capacity:(e + 1) * capacity, :]
            put(r, c, slot).start()

    dispatch(0, None)
    tokens.arrive(tokens.mate)
    dispatch(4, 0)
    tokens.forward()
    dispatch(1, 4)
    dispatch(2, 1)
    gates.arrive(gates.own + gates.mate)
    for copy in gates.near_mate:
        copy.start()
    gates.forward_far()
    tokens.arrive(tokens.near_mate)
    dispatch(5, 2)
    dispatch(6, 5)
    tokens.forward_far()
    gates.arrive(gates.near_mate + gates.far_mate)
    for r in range(group):
        gates_ref[r] = g_buf[r]
    dispatch(3, 6)
    tokens.arrive(tokens.far_mate)
    dispatch(7, 3)
    for c in range(n_cols - 2, n_cols):
        put(7, c, c % 2).wait()
    keep.wait()
    tokens.finish()
    gates.finish()


def dispatch_tokens(h, router_t, ids_t, rank, capacity):
    n_tok, d_model = h.shape
    group, local = rank.shape[:2]
    top_k = ids_t.shape[0]
    width = 512
    vmem = pl.BlockSpec(memory_space=pltpu.VMEM)
    return pl.pallas_call(
        dispatch_kernel,
        in_specs=[vmem] * 4,
        out_specs=[pl.BlockSpec(memory_space=pl.ANY), vmem, pl.BlockSpec(memory_space=pl.ANY)],
        out_shape=[jax.ShapeDtypeStruct((group, local, capacity, d_model), jnp.bfloat16), jax.ShapeDtypeStruct((group, top_k, n_tok), jnp.float32), jax.ShapeDtypeStruct(h.shape, jnp.bfloat16)],
        scratch_shapes=[
            pltpu.VMEM((group, n_tok, d_model), jnp.bfloat16),
            pltpu.VMEM((local * capacity, n_tok), jnp.bfloat16),
            pltpu.VMEM((2, local, capacity, width), jnp.bfloat16),
            pltpu.VMEM((group, top_k, n_tok), jnp.float32),
            pltpu.SemaphoreType.DMA((3,)),
            pltpu.SemaphoreType.DMA((9,)),
            pltpu.SemaphoreType.DMA((9,)),
            pltpu.SemaphoreType.DMA((9,)),
            pltpu.SemaphoreType.DMA((9,)),
        ],
        compiler_params=pltpu.CompilerParams(vmem_limit_bytes=MAX_VMEM, collective_id=1, has_side_effects=True),
        cost_estimate=pl.CostEstimate(flops=2 * group * local * capacity * n_tok * d_model, bytes_accessed=2 * group * local * capacity * d_model, transcendentals=0),
        name="dispatch_tokens",
    )(h, router_t, ids_t, rank)


def expert_kernel(size_ref, start_ref, total_ref, x_ref, gate_ref, up_ref, down_ref, f_ref, x_buf, f_buf, in_sems, out_sems, *, chunk):
    n_src, _, capacity, d_model = x_ref.shape
    e, local = pl.program_id(0), pl.num_programs(0)
    slot = lax.rem(e, 2)
    zeros = jnp.zeros((capacity, d_model), jnp.bfloat16)

    def fetch(r, expert, where):
        size = pl.multiple_of(size_ref[r, expert], ALIGN)
        start = pl.multiple_of(start_ref[r, expert], ALIGN)
        return pltpu.make_async_copy(x_ref.at[r, expert, pl.ds(0, size), :], x_buf.at[where, pl.ds(start, size), :], in_sems.at[where, r])

    def put(r, expert, where):
        start = pl.multiple_of(start_ref[r, expert], ALIGN)
        return pltpu.make_async_copy(f_buf.at[where, pl.ds(start, capacity), :], f_ref.at[r, expert], out_sems.at[where, r])

    @pl.when(e == 0)
    def _():
        for r in range(n_src):
            fetch(r, 0, 0).start()

    @pl.when(e + 1 < local)
    def _():
        for r in range(n_src):
            fetch(r, e + 1, 1 - slot).start()

    for r in range(n_src):
        fetch(r, e, slot).wait()

    @pl.when(e >= 2)
    def _():
        for r in range(n_src):
            put(r, e - 2, slot).wait()

    total = total_ref[e]
    x_buf[slot, pl.ds(pl.multiple_of(total, ALIGN), capacity), :] = zeros
    chunks = (total + chunk - 1) // chunk

    def run(start, size):
        rows = pl.ds(pl.multiple_of(start, chunk), size)
        x = x_buf[slot, rows, :]
        gate_act = jnp.dot(x, gate_ref[0], preferred_element_type=jnp.float32)
        up_act = jnp.dot(x, up_ref[0], preferred_element_type=jnp.float32)
        middle = (gate_act * jax.nn.sigmoid(gate_act) * up_act).astype(jnp.bfloat16)
        f_buf[slot, rows, :] = jnp.dot(middle, down_ref[0], preferred_element_type=jnp.float32).astype(jnp.bfloat16)

    @pl.loop(0, chunks // 2)
    def _(i):
        run(i * 2 * chunk, 2 * chunk)

    @pl.when(lax.rem(chunks, 2) == 1)
    def _():
        run((chunks - 1) * chunk, chunk)

    f_buf[slot, pl.ds(pl.multiple_of(chunks * chunk, chunk), capacity), :] = zeros
    for r in range(n_src):
        put(r, e, slot).start()

    @pl.when(e == local - 1)
    def _():
        @pl.when(e >= 1)
        def _():
            for r in range(n_src):
                put(r, e - 1, 1 - slot).wait()
        for r in range(n_src):
            put(r, e, slot).wait()


def experts(sizes, starts, totals, rows, gate_w, up_w, down_w):
    n_src, local, capacity, d_model = rows.shape
    width = gate_w.shape[2]
    chunk = capacity
    n_rows = n_src * capacity + 2 * capacity
    anywhere = pl.BlockSpec(memory_space=pl.ANY)
    return pl.pallas_call(
        functools.partial(expert_kernel, chunk=chunk),
        grid_spec=pltpu.PrefetchScalarGridSpec(
            num_scalar_prefetch=3,
            grid=(local,),
            in_specs=[anywhere] + [
                pl.BlockSpec((1, d_model, width), lambda e, *_: (e, 0, 0)),
                pl.BlockSpec((1, d_model, width), lambda e, *_: (e, 0, 0)),
                pl.BlockSpec((1, width, d_model), lambda e, *_: (e, 0, 0)),
            ],
            out_specs=anywhere,
            scratch_shapes=[
                pltpu.VMEM((2, n_rows, d_model), jnp.bfloat16),
                pltpu.VMEM((2, n_rows, d_model), jnp.bfloat16),
                pltpu.SemaphoreType.DMA((2, n_src)),
                pltpu.SemaphoreType.DMA((2, n_src)),
            ],
        ),
        out_shape=jax.ShapeDtypeStruct(rows.shape, jnp.bfloat16),
        compiler_params=params(),
        cost_estimate=pl.CostEstimate(flops=4 * local * n_src * capacity * d_model * width, bytes_accessed=6 * local * d_model * width, transcendentals=0),
        name="experts",
    )(sizes, starts, totals, rows, gate_w, up_w, down_w)


def reduce_kernel(rank_ref, ids_ref, gates_ref, f_ref, h_hbm, u_hbm, gate_hbm, up_hbm, down_hbm, out_ref, f_buf, spread, other_buf, swap_buf, send_buf, ring_buf, f_sems, swap_send, swap_recv, ring_send, ring_recv, out_sems, free_sem):
    n_src, local, n_tok = rank_ref.shape
    capacity = f_ref.shape[2]
    top_k = ids_ref.shape[1]
    pieces = spread.shape[1]
    chips = n_src // 2
    width = out_ref.shape[1] // 4
    n_units = 16

    def quarter(u):
        return 2 * lax.rem(u, 2) + u // 2

    def place(i):
        u = lax.rem(i, 4)
        odd = lax.rem(u, 2)
        target = jnp.where(i < 4, 1 + odd, jnp.where(i < 8, 2 - odd, jnp.where(i < 12, 3, 0)))
        return u, target

    def fetch(i, side, slot):
        u, target = place(i)
        cols = pl.ds(pl.multiple_of(quarter(u) * width, width), width)
        return pltpu.make_async_copy(f_ref.at[target + chips * (1 - side), :, :, cols], f_buf.at[slot, side], f_sems.at[slot, side])

    def swap_copy(i):
        s = lax.rem(i, 4)
        return remote(other_buf.at[s], swap_buf.at[s], swap_send.at[s], swap_recv.at[s], neighbour(0, True))

    def ring_copy(source, slot):
        return remote(send_buf.at[source], ring_buf.at[slot], ring_send.at[slot], ring_recv.at[slot], neighbour(1 - 2 * lax.rem(slot, 2)))

    def build(target, entry):
        @pl.loop(0, 2)
        def _(side):
            r = target + chips * (1 - side)
            first = lax.axis_index('ep') * local
            ids = ids_ref[r]
            gates = gates_ref[r]
            rest = jnp.concatenate([jnp.sum(jnp.where(ids == first + e, gates, 0.0), axis=0, keepdims=True) for e in range(local)], axis=0)
            table = [rank_ref[r].astype(jnp.float32)]
            for _ in range(pieces):
                table.append(rest.astype(jnp.bfloat16).astype(jnp.float32))
                rest = rest - table[-1]
            table = jnp.concatenate(table, axis=0).T
            rank = table[:, :local].astype(jnp.int32)
            weights = table[:, local:]
            slots = lax.broadcasted_iota(jnp.int32, (n_tok, capacity), 1)
            for e in range(local):
                hit = rank[:, e:e + 1] == slots
                for k in range(pieces):
                    column = k * local + e
                    spread[entry * 2 + side, k, :, e * capacity:(e + 1) * capacity] = jnp.where(hit, weights[:, column:column + 1], 0.0).astype(jnp.bfloat16)

    def product(entry, slot, side):
        data = jnp.concatenate([f_buf[slot, side, e] for e in range(local)], axis=0)
        total = jnp.dot(spread[entry * 2 + side, 0], data, preferred_element_type=jnp.float32)
        for k in range(1, pieces):
            total += jnp.dot(spread[entry * 2 + side, k], data, preferred_element_type=jnp.float32)
        return total

    for side in range(2):
        fetch(0, side, 0).start()
    greet(neighbour(1), neighbour(-1), neighbour(0, True))

    @pl.loop(0, n_units)
    def _(i):
        u, target = place(i)
        slot = lax.rem(i, 2)
        lane = lax.rem(i, 4)

        @pl.when(i + 1 < n_units)
        def _():
            for side in range(2):
                fetch(i + 1, side, 1 - slot).start()

        @pl.when(i == 0)
        def _():
            build(1, 0)

        @pl.when(i == 1)
        def _():
            build(2, 1)

        @pl.when(i == 8)
        def _():
            build(3, 0)

        @pl.when(i == 12)
        def _():
            build(0, 1)

        entry = 1 - lax.rem(target, 2)

        @pl.when(i >= 4)
        def _():
            swap_copy(i - 4).wait_send()
            pl.semaphore_wait(free_sem, 1)

        fetch(i, 0, slot).wait()
        other_buf[lane] = product(entry, slot, 0)
        swap_copy(i).start()
        fetch(i, 1, slot).wait()
        send_buf[i] = product(entry, slot, 1)
        swap_copy(i).wait_recv()
        send_buf[i] += swap_buf[lane]

        @pl.when(i < n_units - 4)
        def _():
            pl.semaphore_signal(free_sem, inc=1, device_id=neighbour(0, True), device_id_type=pl.DeviceIdType.MESH)

        @pl.when(i < 4)
        def _():
            ring_copy(i, u).start()

        @pl.when((i >= 8) & (i < 12))
        def _():
            ring_copy(i, u).wait_recv()
            send_buf[i] += ring_buf[u]
            ring_copy(i, u + 4).start()

    @pl.loop(0, 4)
    def _(u):
        ring_copy(0, u + 4).wait_recv()
        send_buf[u + 4] += ring_buf[u + 4]
        ring_copy(u + 4, u + 8).start()

    for u in range(4):
        swap_copy(n_units - 4 + u).wait_send()
    half = 2 * width
    loads = []
    for k in range(2):
        cols = pl.ds(k * half, half)
        loads.append(pltpu.make_async_copy(u_hbm.at[:, cols], spread.at[0, 1 + k], out_sems.at[k]))
        loads.append(pltpu.make_async_copy(h_hbm.at[:, cols], spread.at[1, k], out_sems.at[2 + k]))

    def shared_tile(t, side):
        source = (gate_hbm, up_hbm)[side]
        slot = lax.rem(t, 2)
        depth = pl.ds(pl.multiple_of(lax.rem(t, 2) * local, local), local)
        cols = pl.ds(pl.multiple_of(t // 2 * width, width), width)
        return pltpu.make_async_copy(source.at[depth, :, cols], f_buf.at[slot, side], f_sems.at[slot, side])

    def down_tile(q):
        slot = lax.rem(q, 2)
        cols = pl.ds(pl.multiple_of(q * width, width), width)
        return pltpu.make_async_copy(down_hbm.at[:, :, cols], f_buf.at[slot, 0], f_sems.at[slot, 0])

    for load in loads:
        load.start()
    for side in range(2):
        shared_tile(0, side).start()
    for load in loads:
        load.wait()

    @pl.loop(0, 4)
    def _(t):
        @pl.when(t < 3)
        def _():
            for side in range(2):
                shared_tile(t + 1, side).start()

        @pl.when(t == 3)
        def _():
            down_tile(0).start()

        k = lax.rem(t, 2)
        for side in range(2):
            shared_tile(t, side).wait()
            data = jnp.concatenate([f_buf[k, side, e] for e in range(local)], axis=0)
            part = jnp.dot(spread[0, 1 + k], data, preferred_element_type=jnp.float32)

            @pl.when(k == 0)
            def _():
                other_buf[side] = part

            @pl.when(k == 1)
            def _():
                other_buf[side] += part

        @pl.when(k == 1)
        def _():
            gate_act = other_buf[0]
            middle = gate_act * jax.nn.sigmoid(gate_act) * other_buf[1]
            spread[0, 0, :, pl.ds(pl.multiple_of(t // 2 * width, width), width)] = middle.astype(jnp.bfloat16)

    @pl.loop(0, 4)
    def _(q):
        @pl.when(q < 3)
        def _():
            down_tile(q + 1).start()

        down_tile(q).wait()
        data = jnp.concatenate([f_buf[lax.rem(q, 2), 0, e] for e in range(local)], axis=0)
        swap_buf[q] = jnp.dot(spread[0, 0], data, preferred_element_type=jnp.float32).astype(jnp.bfloat16).astype(jnp.float32)

    def put(u):
        q = quarter(u)
        inner = pl.ds(pl.multiple_of(lax.rem(q, 2) * width, width), width)
        cols = pl.ds(pl.multiple_of(q * width, width), width)
        return pltpu.make_async_copy(spread.at[3, q // 2, :, inner], out_ref.at[:, cols], out_sems.at[u])

    @pl.loop(0, 4)
    def _(u):
        q = quarter(u)
        inner = pl.ds(pl.multiple_of(lax.rem(q, 2) * width, width), width)
        ring_copy(0, u + 8).wait_recv()
        routed = send_buf[12 + u] + ring_buf[u + 8]
        spread[3, q // 2, :, inner] = (spread[1, q // 2, :, inner].astype(jnp.float32) + routed + swap_buf[q]).astype(jnp.bfloat16)
        put(u).start()

    @pl.loop(0, 4)
    def _(u):
        put(u).wait()
        ring_copy(u, u).wait_send()
        ring_copy(8 + u, u + 4).wait_send()
        ring_copy(4 + u, u + 8).wait_send()


def reduce_results(rank, ids, gates, results, residual, moe_in, gate_w, up_w, down_w):
    n_src, local, capacity, d_model = results.shape
    n_tok = rank.shape[2]
    width = d_model // 4
    n_pieces = 3
    tile = (n_tok, width)
    vmem = pl.BlockSpec(memory_space=pltpu.VMEM)
    return pl.pallas_call(
        reduce_kernel,
        in_specs=[vmem] * 3 + [pl.BlockSpec(memory_space=pl.ANY)] * 6,
        out_specs=pl.BlockSpec(memory_space=pl.ANY),
        out_shape=jax.ShapeDtypeStruct((n_tok, d_model), jnp.bfloat16),
        scratch_shapes=[
            pltpu.VMEM((2, 2, local, capacity, width), jnp.bfloat16),
            pltpu.VMEM((4, n_pieces, n_tok, local * capacity), jnp.bfloat16),
            pltpu.VMEM((4,) + tile, jnp.float32),
            pltpu.VMEM((4,) + tile, jnp.float32),
            pltpu.VMEM((16,) + tile, jnp.float32),
            pltpu.VMEM((12,) + tile, jnp.float32),
            pltpu.SemaphoreType.DMA((2, 2)),
            pltpu.SemaphoreType.DMA((4,)),
            pltpu.SemaphoreType.DMA((4,)),
            pltpu.SemaphoreType.DMA((12,)),
            pltpu.SemaphoreType.DMA((12,)),
            pltpu.SemaphoreType.DMA((4,)),
            pltpu.SemaphoreType.REGULAR,
        ],
        compiler_params=pltpu.CompilerParams(vmem_limit_bytes=MAX_VMEM, collective_id=2, has_side_effects=True),
        cost_estimate=pl.CostEstimate(flops=6 * n_src * local * capacity * n_tok * d_model, bytes_accessed=4 * n_src * local * capacity * d_model, transcendentals=0),
        name="reduce_results",
    )(rank, ids, gates, results, residual, moe_in, *[w.reshape(-1, capacity, w.shape[1]) for w in (gate_w, up_w, down_w)])


def local_layer(x_loc, q_shard, k_shard, v_shard, o_shard, w_router, gate_loc, up_loc, down_loc, sgate_shard, sup_shard, sdown_shard, ids_loc, group):
    n_seq, seq_len, d_model = x_loc.shape
    assert n_seq == 1 and group == 8 and q_shard.shape[2] == 128
    n_tok = n_seq * seq_len
    top_k = ids_loc.shape[-1]
    local = gate_loc.shape[0]
    n_experts = local * group
    capacity = CAP_FACTOR * n_tok * top_k // n_experts
    def gathered(shard):
        return lax.all_gather(shard.reshape(shard.shape[0], -1), 'ep', axis=0, tiled=True)

    x_flat = x_loc.reshape(n_tok, d_model)
    ids_t = ids_loc.reshape(n_tok, top_k).T
    residual, rank, ids_all = attention_layer(x_flat, ids_t, *[w.reshape(w.shape[0], -1) for w in (k_shard, v_shard, q_shard, o_shard)], group, local)
    rows, gates_all, moe_in = dispatch_tokens(residual, w_router.T, ids_t, rank, capacity)

    sizes = (jnp.max(rank, axis=2) + 1 + ALIGN - 1) // ALIGN * ALIGN
    ends = jnp.cumsum(sizes, axis=0)
    starts, totals = ends - sizes, ends[-1]
    rows, sgate_shard, sup_shard, sdown_shard = lax.optimization_barrier((rows, sgate_shard, sup_shard, sdown_shard))
    results = experts(sizes, starts, totals, rows, gate_loc, up_loc, down_loc)

    y_out = reduce_results(rank, ids_all, gates_all, results, residual, moe_in, gathered(sgate_shard), gathered(sup_shard), gathered(sdown_shard))
    return y_out.reshape(n_seq, seq_len, d_model)


def solution(mesh):
    tok_spec = P(('dp', 'ep'), None, None)
    row_spec = P('ep', None)
    cube_spec = P('ep', None, None)
    in_specs = (tok_spec, cube_spec, cube_spec, cube_spec, row_spec, P(None, None), cube_spec, cube_spec, cube_spec, row_spec, row_spec, row_spec, tok_spec)
    return jax.shard_map(functools.partial(local_layer, group=mesh.shape['ep']), mesh=mesh, in_specs=in_specs, out_specs=tok_spec, check_vma=False)
```

profile of v0, /device:TPU:81, one launch (start us, length us, event | category | flops | bytes accessed | tf_op | source)
XLA Modules:
  0.0 514.9 jit_solution(13506549107594464203)
XLA Ops:
  6.5 0.0 all-gather.4.cloned.1.call-start
  6.6 2.5 copy.20
  9.0 3.4 copy_bitcast_fusion
  12.4 150.5 %attention_layer.1 = (bf16[512,2048]{1,0:T(8,128)(2,1)}, s32[8,8,512]{2,1,0:T(8,128)}, s32[8,8,512]{2,1,0:T(8,128)}) custom-call(bf16[512,2048]{1,0:T(8,128)(2,1)} %bitcast.29, s32[8,512]{1,0:T(8,128)} %bitcast.31, bf16[256,2048]{1,0:T(8,128)(2,1)} %bitcast.23, bf16[256,2048]{1,0:T(8,128)(2,1)} %get-tuple-element.26.v_hbm, ...), custom_call_target="tpu_custom_call" | custom-call | flops 19327352832 | bytes 4194304 | tf_op jit(solution)/shard_map/attention_layer/pallas_call | solution.py:217
  163.0 95.4 %dispatch_tokens.1 = (bf16[8,8,128,2048]{3,2,1,0:T(8,128)(2,1)}, f32[8,8,512]{2,1,0:T(8,128)}, bf16[512,2048]{1,0:T(8,128)(2,1)}) custom-call(bf16[512,2048]{1,0:T(8,128)(2,1)} %get-tuple-element.17.h_ref.h_hbm, f32[64,2048]{1,0:T(8,128)} %bitcast.30, s32[8,512]{1,0:T(8,128)} %bitcast.32, s32[8,8,512]{2,1,0:T(8,128)} %get-tuple-element.15.rank_ref), custom_call_target="tpu_custom_call" | custom-call | flops 17179869184 | bytes 33554432 | tf_op jit(solution)/shard_map/dispatch_tokens/pallas_call | solution.py:333
  258.3 0.1 all-gather.4.cloned.1.call-update
  258.4 0.1 all-gather.6.cloned.1.call-start
  258.5 0.7 all-gather.6.cloned.1.call-update
  259.2 0.1 all-gather.8.cloned.1.call-start
  259.3 0.7 all-gather.8.cloned.1.call-update
  260.0 1.1 reduce_max.9
  261.2 0.0 copy-start
  261.2 0.5 slice_bitcast_fusion.total_ref
  261.7 0.6 fusion.3.start_ref
  262.3 0.0 copy-done
  262.3 74.3 %experts.1.f_ref = bf16[8,8,128,2048]{3,2,1,0:T(8,128)(2,1)} custom-call(s32[8,8]{1,0:T(8,128)} %copy-done, s32[8,8]{1,0:T(8,128)} %fusion.3.start_ref, s32[8]{0:T(128)} %slice_bitcast_fusion.total_ref, bf16[8,8,128,2048]{3,2,1,0:T(8,128)(2,1)} %get-tuple-element.20.x_ref, bf16[8,2048,1024]{2,1,0:T(8,128)(2,1)} %gate_ref.1, bf16[8,2048,1024]{2,1,0:T(8,128)(2,1)} %up_ref.1, ...), custom_call_target="tpu_custom_call" | custom-call | flops 68719476736 | bytes 100663296 | tf_op jit(solution)/shard_map/experts/pallas_call | solution.py:428
  336.6 0.0 all-gather.4.cloned.1.call-done
  336.6 0.0 all-gather.6.cloned.1.call-done
  336.6 13.4 %all-gather.8.cloned.1.call-done = bf16[1024,2048]{1,0:T(8,128)(2,1)} async-done(((bf16[128,2048]{1,0:T(8,128)(2,1)}), bf16[1024,2048]{1,0:T(8,128)(2,1)}) %all-gather.8.cloned.1.call-update) | async-done | bytes 4194320 | tf_op jit(solution)/shard_map/all_gather | solution.py:712
  350.1 154.8 %reduce_results.1 = bf16[512,2048]{1,0:T(8,128)(2,1)} custom-call(s32[8,8,512]{2,1,0:T(8,128)} %get-tuple-element.15.rank_ref, s32[8,8,512]{2,1,0:T(8,128)} %get-tuple-element.16.ids_ref, f32[8,8,512]{2,1,0:T(8,128)} %get-tuple-element.18.gates_ref, bf16[8,8,128,2048]{3,2,1,0:T(8,128)(2,1)} %experts.1.f_ref, ...), custom_call_target="tpu_custom_call" | custom-call | flops 51539607552 | bytes 67108864 | tf_op jit(solution)/shard_map/reduce_results/pallas_call | solution.py:677
  504.9 3.2 copy.22
  (2 shorter events, 0.0 us)
Async XLA Ops:
  6.5 330.1 %all-gather.4.cloned.1.call-start = ((), (), s32[]{:S(2)}) async-start(), calls=%async_computation | async-start | bytes 4718592 | tf_op jit(solution)/shard_map/all_gather | solution.py:712
  258.4 78.2 %all-gather.6.cloned.1.call-start = ((), (), s32[]{:S(2)}) async-start(), calls=%async_computation.1 | async-start | bytes 4718592 | tf_op jit(solution)/shard_map/all_gather | solution.py:712
  259.2 90.8 %all-gather.8.cloned.1.call-start = ((), (), s32[]{:S(2)}) async-start(), calls=%async_computation.2 | async-start | bytes 4718592 | tf_op jit(solution)/shard_map/all_gather | solution.py:712
  261.2 1.2 copy-start
Sparse Core Ops, SparseCore 0:
  258.5 30.9 all-gather.3
  291.1 28.6 all-gather.5
  321.4 28.6 all-gather.7
where the time goes:
time: 518 us; the launch traced here: 515 us
  Pallas kernels  475 us (92%)
  waiting for transfers between devices  15 us (3%)
  between operations  13.6 us (3%)
  local copies, waits for them, and re-layouts  9.55 us (2%)
    pallas_call x1, Pallas kernels, reduce_results(): pl.pallas_call(reduce_kernel, in_specs=[vmem] * 3 + [pl.BlockSpec(memory_...  155 us
    pallas_call x1, Pallas kernels, attention_layer(): pl.pallas_call(attention_layer_kernel, in_specs=[vmem] + [anywhere] * 5,...  151 us
    pallas_call x1, Pallas kernels, dispatch_tokens(): pl.pallas_call(dispatch_kernel, in_specs=[vmem] * 4, out_specs=[pl.BlockS...  95.4 us
    pallas_call x1, Pallas kernels, experts(): pl.pallas_call(functools.partial(expert_kernel, chunk=chunk), grid_spec=p...  74.3 us
    all_gather x3, waiting for transfers between devices, gathered(): lax.all_gather(shard.reshape(shard.shape[0], -1), 'ep', axis=0, tiled=True)  13.5 us
  transfers between devices with their start and end apart: 3, of which 1 were waited for; matrix products, arithmetic and copies ran while one was open for 0% of the time, Pallas kernels for 14%

commit v1 on v0

--- a/solution.py
+++ b/solution.py
@@ -303,20 +303,20 @@
     tokens.forward()
     dispatch(1, 4)
     dispatch(2, 1)
+    tokens.arrive(tokens.near_mate)
+    dispatch(5, 2)
+    dispatch(6, 5)
+    tokens.forward_far()
+    dispatch(3, 6)
     gates.arrive(gates.own + gates.mate)
     for copy in gates.near_mate:
         copy.start()
     gates.forward_far()
-    tokens.arrive(tokens.near_mate)
-    dispatch(5, 2)
-    dispatch(6, 5)
-    tokens.forward_far()
+    tokens.arrive(tokens.far_mate)
+    dispatch(7, 3)
     gates.arrive(gates.near_mate + gates.far_mate)
     for r in range(group):
         gates_ref[r] = g_buf[r]
-    dispatch(3, 6)
-    tokens.arrive(tokens.far_mate)
-    dispatch(7, 3)
     for c in range(n_cols - 2, n_cols):
         put(7, c, c % 2).wait()
     keep.wait()
@@ -450,7 +450,7 @@
     )(sizes, starts, totals, rows, gate_w, up_w, down_w)
 
 
-def reduce_kernel(rank_ref, ids_ref, gates_ref, f_ref, h_hbm, u_hbm, gate_hbm, up_hbm, down_hbm, out_ref, f_buf, spread, other_buf, swap_buf, send_buf, ring_buf, f_sems, swap_send, swap_recv, ring_send, ring_recv, out_sems, free_sem):
+def reduce_kernel(rank_ref, ids_ref, gates_ref, f_ref, h_hbm, u_hbm, pair_hbm, down_hbm, out_ref, f_buf, spread, other_buf, swap_buf, send_buf, ring_buf, f_sems, swap_send, swap_recv, ring_send, ring_recv, out_sems, free_sem):
     n_src, local, n_tok = rank_ref.shape
     capacity = f_ref.shape[2]
     top_k = ids_ref.shape[1]
@@ -585,11 +585,10 @@
         loads.append(pltpu.make_async_copy(h_hbm.at[:, cols], spread.at[1, k], out_sems.at[2 + k]))
 
     def shared_tile(t, side):
-        source = (gate_hbm, up_hbm)[side]
         slot = lax.rem(t, 2)
         depth = pl.ds(pl.multiple_of(lax.rem(t, 2) * local, local), local)
-        cols = pl.ds(pl.multiple_of(t // 2 * width, width), width)
-        return pltpu.make_async_copy(source.at[depth, :, cols], f_buf.at[slot, side], f_sems.at[slot, side])
+        cols = pl.ds(pl.multiple_of((t // 2 + 2 * side) * width, width), width)
+        return pltpu.make_async_copy(pair_hbm.at[depth, :, cols], f_buf.at[slot, side], f_sems.at[slot, side])
 
     def down_tile(q):
         slot = lax.rem(q, 2)
@@ -667,7 +666,7 @@
         ring_copy(4 + u, u + 8).wait_send()
 
 
-def reduce_results(rank, ids, gates, results, residual, moe_in, gate_w, up_w, down_w):
+def reduce_results(rank, ids, gates, results, residual, moe_in, pair_w, down_w):
     n_src, local, capacity, d_model = results.shape
     n_tok = rank.shape[2]
     width = d_model // 4
@@ -676,7 +675,7 @@
     vmem = pl.BlockSpec(memory_space=pltpu.VMEM)
     return pl.pallas_call(
         reduce_kernel,
-        in_specs=[vmem] * 3 + [pl.BlockSpec(memory_space=pl.ANY)] * 6,
+        in_specs=[vmem] * 3 + [pl.BlockSpec(memory_space=pl.ANY)] * 5,
         out_specs=pl.BlockSpec(memory_space=pl.ANY),
         out_shape=jax.ShapeDtypeStruct((n_tok, d_model), jnp.bfloat16),
         scratch_shapes=[
@@ -697,7 +696,7 @@
         compiler_params=pltpu.CompilerParams(vmem_limit_bytes=MAX_VMEM, collective_id=2, has_side_effects=True),
         cost_estimate=pl.CostEstimate(flops=6 * n_src * local * capacity * n_tok * d_model, bytes_accessed=4 * n_src * local * capacity * d_model, transcendentals=0),
         name="reduce_results",
-    )(rank, ids, gates, results, residual, moe_in, *[w.reshape(-1, capacity, w.shape[1]) for w in (gate_w, up_w, down_w)])
+    )(rank, ids, gates, results, residual, moe_in, *[w.reshape(-1, capacity, w.shape[1]) for w in (pair_w, down_w)])
 
 
 def local_layer(x_loc, q_shard, k_shard, v_shard, o_shard, w_router, gate_loc, up_loc, down_loc, sgate_shard, sup_shard, sdown_shard, ids_loc, group):
@@ -719,10 +718,11 @@
     sizes = (jnp.max(rank, axis=2) + 1 + ALIGN - 1) // ALIGN * ALIGN
     ends = jnp.cumsum(sizes, axis=0)
     starts, totals = ends - sizes, ends[-1]
-    rows, sgate_shard, sup_shard, sdown_shard = lax.optimization_barrier((rows, sgate_shard, sup_shard, sdown_shard))
+    pair_shard = jnp.concatenate([sgate_shard, sup_shard], axis=1)
+    rows, pair_shard, sdown_shard = lax.optimization_barrier((rows, pair_shard, sdown_shard))
     results = experts(sizes, starts, totals, rows, gate_loc, up_loc, down_loc)
 
-    y_out = reduce_results(rank, ids_all, gates_all, results, residual, moe_in, gathered(sgate_shard), gathered(sup_shard), gathered(sdown_shard))
+    y_out = reduce_results(rank, ids_all, gates_all, results, residual, moe_in, gathered(pair_shard), gathered(sdown_shard))
     return y_out.reshape(n_seq, seq_len, d_model)
 
 

time: 518 us -> 514 us (level)
  waiting for transfers between devices: 15 us -> 0.83 us
  Pallas kernels: 475 us -> 481 us
    all_gather x3 -> x2, waiting for transfers between devices: 13.5 us -> 0.04 us  [gathered(): lax.all_gather(shard.reshape(shard.shape[0], -1), 'ep', axis=0, tiled=True)]
    pallas_call x1, Pallas kernels: 74.3 us -> 79.9 us  [experts(): pl.pallas_call(functools.partial(expert_kernel, chunk=chunk), grid_spec=p...]
  transfers between devices with their start and end apart: 3 -> 2, of which waited for: 1 -> 0; matrix products, arithmetic and copies ran while one was open for 0% -> 0% of each run, Pallas kernels for 14% -> 16%
where the time goes in v1:
time: 514 us; the launch traced here: 506 us
  Pallas kernels  481 us (94%)
  between operations  13.9 us (3%)
  local copies, waits for them, and re-layouts  8.13 us (2%)
    pallas_call x1, Pallas kernels, reduce_results(): pl.pallas_call(reduce_kernel, in_specs=[vmem] * 3 + [pl.BlockSpec(memory_...  155 us
    pallas_call x1, Pallas kernels, attention_layer(): pl.pallas_call(attention_layer_kernel, in_specs=[vmem] + [anywhere] * 5,...  151 us
    pallas_call x1, Pallas kernels, dispatch_tokens(): pl.pallas_call(dispatch_kernel, in_specs=[vmem] * 4, out_specs=[pl.BlockS...  95.3 us
    pallas_call x1, Pallas kernels, experts(): pl.pallas_call(functools.partial(expert_kernel, chunk=chunk), grid_spec=p...  79.9 us
  transfers between devices with their start and end apart: 2, of which 0 were waited for; matrix products, arithmetic and copies ran while one was open for 0% of the time, Pallas kernels for 16%

profile of v1, /device:TPU:81, one launch (start us, length us, event | category | flops | bytes accessed | tf_op | source)
XLA Modules:
  0.0 506.5 jit_solution(10598117703543580805)
XLA Ops:
  6.5 0.0 copy-start.2
  6.6 0.0 all-gather.5.cloned.1.call-start
  6.6 2.6 copy.20
  9.2 0.0 copy-done.2
  9.2 0.0 copy-done.3
  9.2 1.1 pad_maximum_fusion
  10.3 0.0 copy-done
  10.3 0.0 copy-done.1
  10.3 1.8 copy_bitcast_fusion
  12.1 150.6 %attention_layer.1 = (bf16[512,2048]{1,0:T(8,128)(2,1)}, s32[8,8,512]{2,1,0:T(8,128)}, s32[8,8,512]{2,1,0:T(8,128)}) custom-call(bf16[512,2048]{1,0:T(8,128)(2,1)} %bitcast.27, s32[8,512]{1,0:T(8,128)} %bitcast.29, bf16[256,2048]{1,0:T(8,128)(2,1)} %bitcast.22, bf16[256,2048]{1,0:T(8,128)(2,1)} %get-tuple-element.24.v_hbm, ...), custom_call_target="tpu_custom_call" | custom-call | flops 19327352832 | bytes 4194304 | tf_op jit(solution)/shard_map/attention_layer/pallas_call | solution.py:217
  162.7 95.3 %dispatch_tokens.1 = (bf16[8,8,128,2048]{3,2,1,0:T(8,128)(2,1)}, f32[8,8,512]{2,1,0:T(8,128)}, bf16[512,2048]{1,0:T(8,128)(2,1)}) custom-call(bf16[512,2048]{1,0:T(8,128)(2,1)} %get-tuple-element.16.h_ref.h_hbm, f32[64,2048]{1,0:T(8,128)} %bitcast.28, s32[8,512]{1,0:T(8,128)} %bitcast.30, s32[8,8,512]{2,1,0:T(8,128)} %get-tuple-element.14.rank_ref), custom_call_target="tpu_custom_call" | custom-call | flops 17179869184 | bytes 33554432 | tf_op jit(solution)/shard_map/dispatch_tokens/pallas_call | solution.py:333
  258.0 0.1 all-gather.5.cloned.1.call-update
  258.0 0.1 all-gather.3.cloned.1.call-start
  258.1 0.7 all-gather.3.cloned.1.call-update
  258.9 1.1 reduce_max.9
  260.0 0.0 copy-start.4
  260.0 0.5 slice_bitcast_fusion.total_ref
  260.6 0.6 fusion.3.start_ref
  261.2 0.0 copy-done.4
  261.2 79.9 %experts.1.f_ref = bf16[8,8,128,2048]{3,2,1,0:T(8,128)(2,1)} custom-call(s32[8,8]{1,0:T(8,128)} %copy-done.4, s32[8,8]{1,0:T(8,128)} %fusion.3.start_ref, s32[8]{0:T(128)} %slice_bitcast_fusion.total_ref, bf16[8,8,128,2048]{3,2,1,0:T(8,128)(2,1)} %get-tuple-element.19.x_ref, bf16[8,2048,1024]{2,1,0:T(8,128)(2,1)} %gate_ref.1, bf16[8,2048,1024]{2,1,0:T(8,128)(2,1)} %up_ref.1, ...), custom_call_target="tpu_custom_call" | custom-call | flops 68719476736 | bytes 100663296 | tf_op jit(solution)/shard_map/experts/pallas_call | solution.py:428
  341.1 0.0 all-gather.5.cloned.1.call-done
  341.1 0.0 all-gather.3.cloned.1.call-done
  341.1 155.0 %reduce_results.1 = bf16[512,2048]{1,0:T(8,128)(2,1)} custom-call(s32[8,8,512]{2,1,0:T(8,128)} %get-tuple-element.14.rank_ref, s32[8,8,512]{2,1,0:T(8,128)} %get-tuple-element.15.ids_ref, f32[8,8,512]{2,1,0:T(8,128)} %get-tuple-element.17.gates_ref, bf16[8,8,128,2048]{3,2,1,0:T(8,128)(2,1)} %experts.1.f_ref, ...), custom_call_target="tpu_custom_call" | custom-call | flops 51539607552 | bytes 67108864 | tf_op jit(solution)/shard_map/reduce_results/pallas_call | solution.py:676
  496.1 3.2 copy.22
  (5 shorter events, 0.0 us)
Async XLA Ops:
  6.5 2.6 copy-start.2
  6.5 2.6 copy-start.3
  6.6 334.5 %all-gather.5.cloned.1.call-start = ((), (), s32[]{:S(2)}) async-start(), calls=%async_computation.1 | async-start | bytes 4718592 | tf_op jit(solution)/shard_map/all_gather | solution.py:711
  6.6 3.7 copy-start
  6.6 3.7 copy-start.1
  258.0 83.1 %all-gather.3.cloned.1.call-start = ((), (), s32[]{:S(2)}) async-start(), calls=%async_computation | async-start | bytes 9437184 | tf_op jit(solution)/shard_map/all_gather | solution.py:711
  260.0 1.2 copy-start.4
Sparse Core Ops, SparseCore 0:
  258.2 30.8 all-gather.4
  290.7 46.3 all-gather.2
